TPU v7x, 32 devices: a whole 2x2x4 slice. The times are simulated.
32 devices in a mesh: cfg: 2 (over x), ta: 16 (over z, y, core).
Axes of the slice: x: 2, y: 2, z: 4, core: 2. Of those that a mesh axis runs over, the one named last changes fastest.
Arguments:
- fine_source: bfloat16 [32, 128, 2, 2, 24, 128], P('cfg', 'ta'), parts along dimension 0, may hold values from -24 to 24
- projectors: bfloat16 [32, 128, 2304], P(('cfg', 'ta')), parts along dimension 0, may hold values from -0.21875 to 0.21875
- stencil_links: bfloat16 [32, 8, 48, 864], P(('cfg', 'ta')), parts along dimension 0, may hold values from -0.21875 to 0.21875
- quark_mass: float32 [2], P('cfg'), parts along dimension 0, may hold values from 1.5 to 3
Outputs:
- solution: float32 [32, 8, 96, 128], P(('cfg', 'ta')), parts along dimension 0
- residual: float32 [32, 8, 96, 128], P(('cfg', 'ta')), parts along dimension 0
There are 2 independent parts, one for each index of `cfg`. A program takes and returns all parts, laid end to end along the dimension named above; each array names one. Nothing has to cross between parts.
All inputs are finite; a program needn't handle non-finite values.
Results may differ from a plain program's by a relative error of at most 0.012.
The roundings to bfloat16 on the way count: a program that leaves them out, or rounds other values in their place, can miss the bound.
Values may be sent and summed in bfloat16 or wider, within the bound.
A program may use at most 128 MiB of HBM per device.

v0:
```python
import math

import jax
import jax.numpy as jnp
from jax import lax
from jax.sharding import PartitionSpec as P

LX = 4
LZ = 8
ITERS = 3


def from_behind(value, axis, steps):
    count = lax.axis_size(axis)
    pairs = [(source, (source + steps) % count) for source in range(count)]
    return lax.ppermute(value, axis, pairs)


def real_weights(proj_view):
    proj_re = proj_view[..., 0, :]
    proj_im = proj_view[..., 1, :]
    first_row = jnp.stack([proj_re, proj_im], axis=-4)
    second_row = jnp.stack([-proj_im, proj_re], axis=-4)
    return jnp.stack([first_row, second_row], axis=-5)


def inner_local(left, right, comp_count):
    left_re = left[:, :comp_count]
    left_im = left[:, comp_count:]
    right_re = right[:, :comp_count]
    right_im = right[:, comp_count:]
    return (
        jnp.sum(left_re * right_re + left_im * right_im, axis=(0, 1)),
        jnp.sum(left_re * right_im - left_im * right_re, axis=(0, 1)),
    )


def scaled(vector, factor_re, factor_im, comp_count):
    vector_re = vector[:, :comp_count]
    vector_im = vector[:, comp_count:]
    return jnp.concatenate(
        [
            factor_re * vector_re - factor_im * vector_im,
            factor_re * vector_im + factor_im * vector_re,
        ],
        axis=1,
    )


def shards(fine_source, projectors, stencil_links, quark_mass):
    comp_count = stencil_links.shape[2]
    null_count = comp_count // 2
    site_count = stencil_links.shape[1]
    column_count = projectors.shape[1]
    block_count = column_count // site_count
    fine_count = fine_source.shape[4]
    rhs_count = fine_source.shape[5]
    plane_count = fine_source.shape[0]
    moved_proj = lax.all_to_all(projectors, "ta", split_axis=1, concat_axis=0, tiled=True)
    local_columns = fine_source.shape[1]
    group_size = math.gcd(block_count, local_columns)
    groups = local_columns // group_size
    weights = real_weights(
        moved_proj.reshape(plane_count, groups, group_size, 2, null_count, 2, fine_count)
    )
    fine_local = fine_source.reshape(plane_count, groups, group_size, 2, 2, fine_count, rhs_count)
    partial_sums = jnp.einsum(
        "pmgdchvk,pmgchkr->pmdhvr", weights, fine_local, preferred_element_type=jnp.float32
    )
    partial_sums = partial_sums.reshape(plane_count, groups, 2 * comp_count, rhs_count)
    collected = lax.all_to_all(partial_sums, "ta", split_axis=0, concat_axis=1, tiled=True)
    source = jnp.sum(
        collected.reshape(site_count, block_count // group_size, 2 * comp_count, rhs_count), axis=1
    )
    link_view = stencil_links.reshape(site_count, comp_count, 9, 2, comp_count)
    link_re = link_view[:, :, :, 0, :]
    link_im = link_view[:, :, :, 1, :]
    upper_rows = jnp.stack([link_re, -link_im], axis=3)
    lower_rows = jnp.stack([link_im, link_re], axis=3)
    real_operator = jnp.stack([upper_rows, lower_rows], axis=1).reshape(
        site_count, 2 * comp_count, 18 * comp_count
    )
    mass_value = quark_mass[0]
    z_position = lax.axis_index("ta") % LZ
    line_count = site_count // LX

    def flatten_sites(shifted):
        return shifted.reshape(site_count, 2 * comp_count, rhs_count)

    solution = jnp.zeros_like(source)
    residual = source
    basis_q = []
    basis_p = []
    for iteration in range(ITERS):
        direction = residual
        rounded = residual.astype(jnp.bfloat16)
        plane_view = rounded.reshape(line_count, LX, 2 * comp_count, rhs_count)
        x_plus = flatten_sites(jnp.roll(plane_view, -1, axis=1))
        x_minus = flatten_sites(jnp.roll(plane_view, 1, axis=1))
        y_plus = flatten_sites(jnp.roll(plane_view, -1, axis=0))
        y_minus = flatten_sites(jnp.roll(plane_view, 1, axis=0))
        z_plus_near = from_behind(rounded, "ta", -1)
        z_minus_near = from_behind(rounded, "ta", 1)
        upper_pair = from_behind(jnp.stack([rounded, z_minus_near], axis=0), "ta", -LZ)
        lower_pair = from_behind(jnp.stack([rounded, z_plus_near], axis=0), "ta", LZ)
        t_plus = upper_pair[0]
        t_minus = lower_pair[0]
        z_plus = jnp.where(z_position == LZ - 1, lower_pair[1], z_plus_near)
        z_minus = jnp.where(z_position == 0, upper_pair[1], z_minus_near)
        stacked = jnp.stack(
            [rounded, x_plus, x_minus, y_plus, y_minus, z_plus, z_minus, t_plus, t_minus], axis=1
        )
        stacked = stacked.reshape(site_count, 18 * comp_count, rhs_count)
        product = jnp.einsum(
            "sij,sjr->sir", real_operator, stacked, preferred_element_type=jnp.float32
        )
        mapped = product + mass_value * rounded.astype(jnp.float32)
        square_loc = inner_local(mapped, mapped, comp_count)[0]
        cross_re, cross_im = inner_local(mapped, residual, comp_count)
        if iteration > 0:
            coef_pairs = [inner_local(earlier, mapped, comp_count) for earlier in basis_q]
            back_pairs = [inner_local(earlier, residual, comp_count) for earlier in basis_q]
            coef_re = jnp.stack([pair[0] for pair in coef_pairs])
            coef_im = jnp.stack([pair[1] for pair in coef_pairs])
            back_re = jnp.stack([pair[0] for pair in back_pairs])
            back_im = jnp.stack([pair[1] for pair in back_pairs])
        else:
            coef_re = jnp.zeros((1, rhs_count), jnp.float32)
            coef_im = jnp.zeros((1, rhs_count), jnp.float32)
            back_re = jnp.zeros((1, rhs_count), jnp.float32)
            back_im = jnp.zeros((1, rhs_count), jnp.float32)
        square_all, cross_re, cross_im, coef_re, coef_im, back_re, back_im = lax.psum(
            (square_loc, cross_re, cross_im, coef_re, coef_im, back_re, back_im), "ta"
        )
        squared = square_all
        proj_re = cross_re
        proj_im = cross_im
        for number in range(iteration):
            mapped = mapped - scaled(basis_q[number], coef_re[number], coef_im[number], comp_count)
            direction = direction - scaled(
                basis_p[number], coef_re[number], coef_im[number], comp_count
            )
            squared = squared - (
                coef_re[number] * coef_re[number] + coef_im[number] * coef_im[number]
            )
            proj_re = proj_re - (
                coef_re[number] * back_re[number] + coef_im[number] * back_im[number]
            )
            proj_im = proj_im - (
                coef_re[number] * back_im[number] - coef_im[number] * back_re[number]
            )
        factor = 1.0 / jnp.sqrt(squared + 1e-06)
        unit_q = mapped * factor
        unit_p = direction * factor
        alpha_re = proj_re * factor
        alpha_im = proj_im * factor
        solution = solution + scaled(unit_p, alpha_re, alpha_im, comp_count)
        residual = residual - scaled(unit_q, alpha_re, alpha_im, comp_count)
        basis_q.append(unit_q)
        basis_p.append(unit_p)
    return (
        solution.reshape(1, site_count, 2 * comp_count, rhs_count),
        residual.reshape(1, site_count, 2 * comp_count, rhs_count),
    )


def solution(mesh):
    return jax.shard_map(
        shards,
        mesh=mesh,
        in_specs=(
            P("cfg", "ta", None, None, None, None),
            P(("cfg", "ta"), None, None),
            P(("cfg", "ta"), None, None, None),
            P("cfg"),
        ),
        out_specs=(P(("cfg", "ta"), None, None, None), P(("cfg", "ta"), None, None, None)),
        check_vma=False,
    )
```

profile of v0, /device:TPU:0, one launch (start us, length us, event | category | flops | bytes accessed | tf_op | source)
XLA Modules:
  0.0 329.3 jit_solution(6759608211472331523)
XLA Ops:
  4.3 6.0 %reduce.2 = bf16[128,2304]{1,0:T(8,128)(2,1)} reduce(bf16[128,1,2304]{2,1,0:T(2,128)(2,1)} %bitcast.350, bf16[]{:T(256)} %broadcast.28), dimensions={1}, to_apply=%bitcast.316.reduce_sub_computation | reduce | bytes 1179650
  12.9 7.6 %all-to-all-start = ((bf16[16,2,9216]{2,1,0:T(2,128)(2,1)}), bf16[16,2,9216]{2,1,0:T(2,128)(2,1)}, u32[]{:S(2)}, u32[]{:S(2)}) async-start(bf16[16,2,9216]{2,1,0:T(2,128)(2,1)} %reshape.414), calls=%async_computation | async-start | bytes 1179648 | tf_op jit(solution)/shard_map/all_to_all | solution.py:59
  20.5 4.5 %reshape.398 = bf16[8,48,9,2,48]{4,3,2,1,0:T(2,128)(2,1)} reshape(bf16[1,8,48,864]{3,2,1,0:T(8,128)(2,1)} %param.6) | data formatting | bytes 1327104 | tf_op jit(solution)/shard_map/reshape | solution.py:75
  25.0 8.0 %slice_negate_fusion = (bf16[8,48,9,1,48]{4,3,2,1,0:T(2,128)(2,1)}, bf16[8,48,9,1,48]{4,3,2,1,0:T(2,128)(2,1)}, bf16[8,48,9,1,48]{4,3,2,1,0:T(2,128)(2,1)}) fusion(bf16[8,48,9,2,48]{4,3,2,1,0:T(2,128)(2,1)} %reshape.398), kind=kLoop, calls=%fused_computation.198 | loop fusion | flops 165888 | bytes 1658880 | tf_op jit(solution)/shard_map/neg | solution.py:78
  39.4 5.5 %bitcast_reduce_fusion.1 = bf16[128,2304]{1,0:T(8,128)(2,1)} fusion(bf16[128,1,2304]{2,1,0:T(2,128)(2,1)} %reshape.415), kind=kLoop, calls=%fused_computation.209 | loop fusion | bytes 1179648 | tf_op jit(solution)/shard_map/all_to_all | solution.py:59
  44.9 11.4 %reshape.400 = bf16[16,1,8,2,24,2,24]{6,5,4,3,2,0,1:T(2,128)(2,1)} reshape(bf16[128,2304]{1,0:T(8,128)(2,1)} %bitcast_reduce_fusion.1) | data formatting | bytes 1179648 | tf_op jit(solution)/shard_map/reshape | solution.py:64
  56.3 8.3 %fusion.61 = (bf16[16,1,8,2,24,1,24]{6,5,4,3,2,0,1:T(2,128)(2,1)S(1)}, bf16[16,1,8,2,24,1,24]{6,5,4,3,2,0,1:T(2,128)(2,1)S(1)}) fusion(bf16[16,1,8,2,24,2,24]{6,5,4,3,2,0,1:T(2,128)(2,1)} %reshape.400), kind=kLoop, calls=%fused_computation.202 | loop fusion | bytes 1179648 | tf_op jit(solution)/shard_map/slice | solution.py:21
  71.3 4.5 %all-to-all-start.1 = ((f32[16,1,96,128]{3,2,1,0:T(8,128)}), f32[16,1,96,128]{3,2,1,0:T(8,128)}, u32[]{:S(2)}, u32[]{:S(2)}) async-start(f32[16,1,96,128]{3,2,1,0:T(8,128)} %bitcast.16), calls=%async_computation.1 | async-start | bytes 1572864 | tf_op jit(solution)/shard_map/all_to_all | solution.py:71
  75.8 11.0 %maximum_bitcast_fusion.4 = (bf16[8,1,48,9,2,48]{5,4,3,2,1,0:T(2,128)(2,1)S(1)}, bf16[8,1,48,9,2,48]{5,4,3,2,1,0:T(2,128)(2,1)S(1)}) fusion(bf16[8,48,9,1,48]{4,3,2,1,0:T(2,128)(2,1)} %get-tuple-element.58, bf16[8,48,9,1,48]{4,3,2,1,0:T(2,128)(2,1)} %get-tuple-element.60, bf16[8,48,9,1,48]{4,3,2,1,0:T(2,128)(2,1)} %get-tuple-element.59), kind=kLoop, calls=%fused_computation.8 | loop fusion | flops 2654208 | bytes 2322432 | tf_op jit(solution)/shard_map/stack | solution.py:80
  86.9 7.6 %pad_maximum_fusion = bf16[8,2,48,9,2,48]{5,4,3,2,1,0:T(2,128)(2,1)} fusion(bf16[8,1,48,9,2,48]{5,4,3,2,1,0:T(2,128)(2,1)S(1)} %get-tuple-element.57, bf16[8,1,48,9,2,48]{5,4,3,2,1,0:T(2,128)(2,1)S(1)} %get-tuple-element.56), kind=kLoop, calls=%fused_computation.4 | loop fusion | flops 663552 | bytes 2654208 | tf_op jit(solution)/shard_map/stack | solution.py:80
  94.5 6.1 %reshape.399 = bf16[8,96,864]{2,1,0:T(8,128)(2,1)S(1)} reshape(bf16[8,2,48,9,2,48]{5,4,3,2,1,0:T(2,128)(2,1)} %pad_maximum_fusion) | data formatting | bytes 2654208 | tf_op jit(solution)/shard_map/reshape | solution.py:80
  102.7 4.4 %collective-permute-start = (bf16[8,96,128]{2,1,0:T(8,128)(2,1)S(1)}, bf16[8,96,128]{2,1,0:T(8,128)(2,1)S(1)}, u32[]{:S(2)}, u32[]{:S(2)}) collective-permute-start(bf16[8,96,128]{2,1,0:T(8,128)(2,1)S(1)} %get-tuple-element.109), channel_id=1, source_target_pairs={{0,15},{1,0},{2,1},{3,2},{4,3},{5,4},{6,5},{7,6},{8,7},{9,8},{10,9... | collective-permute-start | bytes 589832 | tf_op jit(solution)/shard_map/ppermute | solution.py:16
  110.3 4.9 %collective-permute-done.2 = bf16[8,96,128]{2,1,0:T(8,128)(2,1)S(1)} collective-permute-done((bf16[8,96,128]{2,1,0:T(8,128)(2,1)S(1)}, bf16[8,96,128]{2,1,0:T(8,128)(2,1)S(1)}, u32[]{:S(2)}, u32[]{:S(2)}) %collective-permute-start.2) | collective-permute-done | bytes 196640 | tf_op jit(solution)/shard_map/ppermute | solution.py:16
  118.4 21.5 %collective-permute-done.1 = bf16[2,8,96,128]{3,2,1,0:T(8,128)(2,1)S(1)} collective-permute-done((bf16[2,8,96,128]{3,2,1,0:T(8,128)(2,1)S(1)}, bf16[2,8,96,128]{3,2,1,0:T(8,128)(2,1)S(1)}, u32[]{:S(2)}, u32[]{:S(2)}) %collective-permute-start.1) | collective-permute-done | bytes 393248 | tf_op jit(solution)/shard_map/ppermute | solution.py:16
  140.0 7.2 %collective-permute-done.3 = bf16[2,8,96,128]{3,2,1,0:T(8,128)(2,1)S(1)} collective-permute-done((bf16[2,8,96,128]{3,2,1,0:T(8,128)(2,1)S(1)}, bf16[2,8,96,128]{3,2,1,0:T(8,128)(2,1)S(1)}, u32[]{:S(2)}, u32[]{:S(2)}) %collective-permute-start.3) | collective-permute-done | bytes 393248 | tf_op jit(solution)/shard_map/ppermute | solution.py:16
  148.8 32.8 %all-reduce.2 = (f32[128]{0:T(128)S(1)}, f32[128]{0:T(128)S(1)}, f32[128]{0:T(128)S(1)}) all-reduce(f32[128]{0:T(128)S(1)} %get-tuple-element.28, f32[128]{0:T(128)S(1)} %get-tuple-element.19, f32[128]{0:T(128)S(1)} %get-tuple-element.18), channel_id=1, replica_groups=mesh['cfg'=2,'ta'=16] {'ta'}, use_global_device_ids=true, to_apply=%region_4.5 | all-reduce | flops 384 | bytes 3072 | tf_op jit(solution)/shard_map/psum | solution.py:132
  187.1 6.8 %collective-permute-done.6 = bf16[8,96,128]{2,1,0:T(8,128)(2,1)S(1)} collective-permute-done((bf16[8,96,128]{2,1,0:T(8,128)(2,1)S(1)}, bf16[8,96,128]{2,1,0:T(8,128)(2,1)S(1)}, u32[]{:S(2)}, u32[]{:S(2)}) %collective-permute-start.6) | collective-permute-done | bytes 196640 | tf_op jit(solution)/shard_map/ppermute | solution.py:16
  197.1 14.7 %collective-permute-done.5 = bf16[2,8,96,128]{3,2,1,0:T(8,128)(2,1)S(1)} collective-permute-done((bf16[2,8,96,128]{3,2,1,0:T(8,128)(2,1)S(1)}, bf16[2,8,96,128]{3,2,1,0:T(8,128)(2,1)S(1)}, u32[]{:S(2)}, u32[]{:S(2)}) %collective-permute-start.5) | collective-permute-done | bytes 393248 | tf_op jit(solution)/shard_map/ppermute | solution.py:16
  211.8 8.3 %collective-permute-done.7 = bf16[2,8,96,128]{3,2,1,0:T(8,128)(2,1)S(1)} collective-permute-done((bf16[2,8,96,128]{3,2,1,0:T(8,128)(2,1)S(1)}, bf16[2,8,96,128]{3,2,1,0:T(8,128)(2,1)S(1)}, u32[]{:S(2)}, u32[]{:S(2)}) %collective-permute-start.7) | collective-permute-done | bytes 393248 | tf_op jit(solution)/shard_map/ppermute | solution.py:16
  221.2 31.6 %all-reduce.1 = (f32[128]{0:T(128)S(1)}, f32[128]{0:T(128)S(1)}, f32[128]{0:T(128)}, f32[128]{0:T(128)}, f32[128]{0:T(128)}, /*index=5*/f32[128]{0:T(128)}, f32[128]{0:T(128)}) all-reduce(f32[128]{0:T(128)S(1)} %get-tuple-element.73, f32[128]{0:T(128)S(1)} %get-tuple-element.72, ...), channel_id=1, replica_groups=mesh['cfg'=2,'ta'=16] {'ta'}, use_global_device_ids=true, to_apply=%region_14.15 | all-reduce | flops 896 | bytes 7168 | tf_op jit(solution)/shard_map/psum | solution.py:132
  257.5 6.8 %collective-permute-done.10 = bf16[8,96,128]{2,1,0:T(8,128)(2,1)S(1)} collective-permute-done((bf16[8,96,128]{2,1,0:T(8,128)(2,1)S(1)}, bf16[8,96,128]{2,1,0:T(8,128)(2,1)S(1)}, u32[]{:S(2)}, u32[]{:S(2)}) %collective-permute-start.10) | collective-permute-done | bytes 196640 | tf_op jit(solution)/shard_map/ppermute | solution.py:16
  267.6 17.0 %collective-permute-done.9 = bf16[2,8,96,128]{3,2,1,0:T(8,128)(2,1)S(1)} collective-permute-done((bf16[2,8,96,128]{3,2,1,0:T(8,128)(2,1)S(1)}, bf16[2,8,96,128]{3,2,1,0:T(8,128)(2,1)S(1)}, u32[]{:S(2)}, u32[]{:S(2)}) %collective-permute-start.9) | collective-permute-done | bytes 393248 | tf_op jit(solution)/shard_map/ppermute | solution.py:16
  284.6 8.3 %collective-permute-done.11 = bf16[2,8,96,128]{3,2,1,0:T(8,128)(2,1)S(1)} collective-permute-done((bf16[2,8,96,128]{3,2,1,0:T(8,128)(2,1)S(1)}, bf16[2,8,96,128]{3,2,1,0:T(8,128)(2,1)S(1)}, u32[]{:S(2)}, u32[]{:S(2)}) %collective-permute-start.11) | collective-permute-done | bytes 393248 | tf_op jit(solution)/shard_map/ppermute | solution.py:16
  294.2 30.4 %all-reduce = (f32[2,128]{1,0:T(2,128)S(1)}, f32[2,128]{1,0:T(2,128)S(1)}, f32[128]{0:T(128)S(1)}, f32[128]{0:T(128)S(1)}, f32[2,128]{1,0:T(2,128)S(1)}, /*index=5*/f32[2,128]{1,0:T(2,128)S(1)}, f32[128]{0:T(128)S(1)}) all-reduce(f32[2,128]{1,0:T(2,128)S(1)} %pad_maximum_fusion.18, ...), channel_id=1, replica_groups=mesh['cfg'=2,'ta'=16] {'ta'}, use_global_device_ids=true, to_apply=%region_31.32 | all-reduce | flops 1408 | bytes 11264 | tf_op jit(solution)/shard_map/psum | solution.py:132
  (161 shorter events, 51.5 us)
Async XLA Ops:
  0.6 65.8 %copy-start = (bf16[16,8,2,2,24,128]{5,4,3,2,1,0:T(8,128)(2,1)S(1)}, bf16[16,8,2,2,24,128]{5,4,3,2,1,0:T(8,128)(2,1)}, u32[]{:S(2)}) copy-start(bf16[16,8,2,2,24,128]{5,4,3,2,1,0:T(8,128)(2,1)} %param.4) | copy-start | bytes 9437188
  12.9 23.1 %all-to-all-start = ((bf16[16,2,9216]{2,1,0:T(2,128)(2,1)}), bf16[16,2,9216]{2,1,0:T(2,128)(2,1)}, u32[]{:S(2)}, u32[]{:S(2)}) async-start(bf16[16,2,9216]{2,1,0:T(2,128)(2,1)} %reshape.414), calls=%async_computation | async-start | bytes 1179648 | tf_op jit(solution)/shard_map/all_to_all | solution.py:59
  71.3 30.0 %all-to-all-start.1 = ((f32[16,1,96,128]{3,2,1,0:T(8,128)}), f32[16,1,96,128]{3,2,1,0:T(8,128)}, u32[]{:S(2)}, u32[]{:S(2)}) async-start(f32[16,1,96,128]{3,2,1,0:T(8,128)} %bitcast.16), calls=%async_computation.1 | async-start | bytes 1572864 | tf_op jit(solution)/shard_map/all_to_all | solution.py:71
  102.7 7.5 %collective-permute-start = (bf16[8,96,128]{2,1,0:T(8,128)(2,1)S(1)}, bf16[8,96,128]{2,1,0:T(8,128)(2,1)S(1)}, u32[]{:S(2)}, u32[]{:S(2)}) collective-permute-start(bf16[8,96,128]{2,1,0:T(8,128)(2,1)S(1)} %get-tuple-element.109), channel_id=1, source_target_pairs={{0,15},{1,0},{2,1},{3,2},{4,3},{5,4},{6,5},{7,6},{8,7},{9,8},{10,9... | collective-permute-start | bytes 589832 | tf_op jit(solution)/shard_map/ppermute | solution.py:16
  107.1 8.1 %collective-permute-start.2 = (bf16[8,96,128]{2,1,0:T(8,128)(2,1)S(1)}, bf16[8,96,128]{2,1,0:T(8,128)(2,1)S(1)}, u32[]{:S(2)}, u32[]{:S(2)}) collective-permute-start(bf16[8,96,128]{2,1,0:T(8,128)(2,1)S(1)} %get-tuple-element.109), channel_id=1, source_target_pairs={{0,1},{1,2},{2,3},{3,4},{4,5},{5,6},{6,7},{7,8},{8,9},{9,10},{10,1... | collective-permute-start | bytes 589832 | tf_op jit(solution)/shard_map/ppermute | solution.py:16
  115.3 24.6 %collective-permute-start.1 = (bf16[2,8,96,128]{3,2,1,0:T(8,128)(2,1)S(1)}, bf16[2,8,96,128]{3,2,1,0:T(8,128)(2,1)S(1)}, u32[]{:S(2)}, u32[]{:S(2)}) collective-permute-start(bf16[2,8,96,128]{3,2,1,0:T(8,128)(2,1)S(1)} %get-tuple-element.127), channel_id=1, source_target_pairs={{0,8},{1,9},{2,10},{3,11},{4,12},{5,13},{6,14},{7,15},{8,0},{9,1},... | collective-permute-start | bytes 1179656 | tf_op jit(solution)/shard_map/ppermute | solution.py:16
  115.4 31.8 %collective-permute-start.3 = (bf16[2,8,96,128]{3,2,1,0:T(8,128)(2,1)S(1)}, bf16[2,8,96,128]{3,2,1,0:T(8,128)(2,1)S(1)}, u32[]{:S(2)}, u32[]{:S(2)}) collective-permute-start(bf16[2,8,96,128]{3,2,1,0:T(8,128)(2,1)S(1)} %get-tuple-element.126), channel_id=1, source_target_pairs={{0,8},{1,9},{2,10},{3,11},{4,12},{5,13},{6,14},{7,15},{8,0},{9,1},... | collective-permute-start | bytes 1179656 | tf_op jit(solution)/shard_map/ppermute | solution.py:16
  182.8 72.1 %copy-start.2 = (f32[8,48,128]{2,1,0:T(8,128)}, f32[8,48,128]{2,1,0:T(8,128)S(1)}, u32[]{:S(2)}) copy-start(f32[8,48,128]{2,1,0:T(8,128)S(1)} %get-tuple-element.97) | copy-start | bytes 589828
  182.8 72.1 %copy-start.4 = (f32[8,48,128]{2,1,0:T(8,128)}, f32[8,48,128]{2,1,0:T(8,128)S(1)}, u32[]{:S(2)}) copy-start(f32[8,48,128]{2,1,0:T(8,128)S(1)} %get-tuple-element.98) | copy-start | bytes 589828
  183.8 3.3 collective-permute-start.4
  183.9 10.0 %collective-permute-start.6 = (bf16[8,96,128]{2,1,0:T(8,128)(2,1)S(1)}, bf16[8,96,128]{2,1,0:T(8,128)(2,1)S(1)}, u32[]{:S(2)}, u32[]{:S(2)}) collective-permute-start(bf16[8,96,128]{2,1,0:T(8,128)(2,1)S(1)} %get-tuple-element.50), channel_id=1, source_target_pairs={{0,1},{1,2},{2,3},{3,4},{4,5},{5,6},{6,7},{7,8},{8,9},{9,10},{10,1... | collective-permute-start | bytes 589832 | tf_op jit(solution)/shard_map/ppermute | solution.py:16
  193.9 17.8 %collective-permute-start.5 = (bf16[2,8,96,128]{3,2,1,0:T(8,128)(2,1)S(1)}, bf16[2,8,96,128]{3,2,1,0:T(8,128)(2,1)S(1)}, u32[]{:S(2)}, u32[]{:S(2)}) collective-permute-start(bf16[2,8,96,128]{3,2,1,0:T(8,128)(2,1)S(1)} %get-tuple-element.119), channel_id=1, source_target_pairs={{0,8},{1,9},{2,10},{3,11},{4,12},{5,13},{6,14},{7,15},{8,0},{9,1},... | collective-permute-start | bytes 1179656 | tf_op jit(solution)/shard_map/ppermute | solution.py:16
  194.1 26.0 %collective-permute-start.7 = (bf16[2,8,96,128]{3,2,1,0:T(8,128)(2,1)S(1)}, bf16[2,8,96,128]{3,2,1,0:T(8,128)(2,1)S(1)}, u32[]{:S(2)}, u32[]{:S(2)}) collective-permute-start(bf16[2,8,96,128]{3,2,1,0:T(8,128)(2,1)S(1)} %get-tuple-element.118), channel_id=1, source_target_pairs={{0,8},{1,9},{2,10},{3,11},{4,12},{5,13},{6,14},{7,15},{8,0},{9,1},... | collective-permute-start | bytes 1179656 | tf_op jit(solution)/shard_map/ppermute | solution.py:16
  253.6 40.2 %copy-start.10 = (f32[8,96,128]{2,1,0:T(8,128)}, f32[8,96,128]{2,1,0:T(8,128)S(1)}, u32[]{:S(2)}) copy-start(f32[8,96,128]{2,1,0:T(8,128)S(1)} %fusion.9) | copy-start | bytes 1179652
  253.7 40.1 %copy-start.12 = (f32[8,96,128]{2,1,0:T(8,128)}, f32[8,96,128]{2,1,0:T(8,128)S(1)}, u32[]{:S(2)}) copy-start(f32[8,96,128]{2,1,0:T(8,128)S(1)} %get-tuple-element.49) | copy-start | bytes 1179652
  254.2 3.2 collective-permute-start.8
  254.3 10.0 %collective-permute-start.10 = (bf16[8,96,128]{2,1,0:T(8,128)(2,1)S(1)}, bf16[8,96,128]{2,1,0:T(8,128)(2,1)S(1)}, u32[]{:S(2)}, u32[]{:S(2)}) collective-permute-start(bf16[8,96,128]{2,1,0:T(8,128)(2,1)S(1)} %get-tuple-element.48), channel_id=1, source_target_pairs={{0,1},{1,2},{2,3},{3,4},{4,5},{5,6},{6,7},{7,8},{8,9},{9,10},{10,1... | collective-permute-start | bytes 589832 | tf_op jit(solution)/shard_map/ppermute | solution.py:16
  264.4 20.2 %collective-permute-start.9 = (bf16[2,8,96,128]{3,2,1,0:T(8,128)(2,1)S(1)}, bf16[2,8,96,128]{3,2,1,0:T(8,128)(2,1)S(1)}, u32[]{:S(2)}, u32[]{:S(2)}) collective-permute-start(bf16[2,8,96,128]{3,2,1,0:T(8,128)(2,1)S(1)} %get-tuple-element.111), channel_id=1, source_target_pairs={{0,8},{1,9},{2,10},{3,11},{4,12},{5,13},{6,14},{7,15},{8,0},{9,1},... | collective-permute-start | bytes 1179656 | tf_op jit(solution)/shard_map/ppermute | solution.py:16
  264.5 28.4 %collective-permute-start.11 = (bf16[2,8,96,128]{3,2,1,0:T(8,128)(2,1)S(1)}, bf16[2,8,96,128]{3,2,1,0:T(8,128)(2,1)S(1)}, u32[]{:S(2)}, u32[]{:S(2)}) collective-permute-start(bf16[2,8,96,128]{3,2,1,0:T(8,128)(2,1)S(1)} %get-tuple-element.110), channel_id=1, source_target_pairs={{0,8},{1,9},{2,10},{3,11},{4,12},{5,13},{6,14},{7,15},{8,0},{9,1},... | collective-permute-start | bytes 1179656 | tf_op jit(solution)/shard_map/ppermute | solution.py:16
  293.8 30.8 %copy-start.15 = (f32[8,96,128]{2,1,0:T(8,128)}, f32[8,96,128]{2,1,0:T(8,128)S(1)}, u32[]{:S(2)}) copy-start(f32[8,96,128]{2,1,0:T(8,128)S(1)} %convolution_add_fusion) | copy-start | bytes 1179652
  293.8 30.9 %copy-start.17 = (f32[8,96,128]{2,1,0:T(8,128)S(1)}, f32[8,96,128]{2,1,0:T(8,128)}, u32[]{:S(2)}) copy-start(f32[8,96,128]{2,1,0:T(8,128)} %get-tuple-element.107) | copy-start | bytes 1179652
  293.8 30.9 %copy-start.21 = (f32[128]{0:T(128)S(1)}, f32[128]{0:T(128)}, u32[]{:S(2)}) copy-start(f32[128]{0:T(128)} %copy-done.20) | copy-start | bytes 1540
  293.8 30.9 %copy-start.23 = (f32[128]{0:T(128)S(1)}, f32[128]{0:T(128)}, u32[]{:S(2)}) copy-start(f32[128]{0:T(128)} %copy-done.22) | copy-start | bytes 1540
  293.8 31.0 %copy-start.19 = (f32[128]{0:T(128)S(1)}, f32[128]{0:T(128)}, u32[]{:S(2)}) copy-start(f32[128]{0:T(128)} %copy-done.18) | copy-start | bytes 1540
  (14 other events, 18.0 us)
where the time goes:
time: 335 us; the launch traced here: 329 us
  waiting for transfers between devices  106 us (32%)
  blocking collectives  94.8 us (28%)
  local copies, waits for them, and re-layouts  51 us (15%)
  other arithmetic  42.2 us (13%)
  starting transfers between devices  27 us (8%)
  matrix products  5.66 us (2%)
    ppermute x12, waiting for transfers between devices, from_behind(): return lax.ppermute(value, axis, pairs)  103 us
    psum x3, blocking collectives, shards(): lax.psum((square_loc, cross_re, cross_im, coef_re, coef_im, back_re, back...  94.8 us
    another operation x2, other arithmetic, shards(): jnp.stack([upper_rows, lower_rows], axis=1)  18.6 us
    ppermute x12, starting transfers between devices, from_behind(): return lax.ppermute(value, axis, pairs)  14.8 us
    unnamed x68, local copies, waits for them, and re-layouts  13.5 us
    reshape x1, local copies, waits for them, and re-layouts, shards(): moved_proj.reshape(plane_count, groups, group_size, 2, null_count, 2, fin...  11.4 us
    slice x1, local copies, waits for them, and re-layouts, real_weights(): proj_im = proj_view[..., 1, :]  8.34 us
    neg x1, other arithmetic, shards(): upper_rows = jnp.stack([link_re, -link_im], axis=3)  8.01 us
  transfers between devices with their start and end apart: 14, of which 13 were waited for; matrix products, arithmetic and copies ran while one was open for 12% of the time, Pallas kernels for 0%

commit v1 on v0

--- a/solution.py
+++ b/solution.py
@@ -1,8 +1,11 @@
+import functools
 import math
 
 import jax
 import jax.numpy as jnp
 from jax import lax
+from jax.experimental import pallas as pl
+from jax.experimental.pallas import tpu as pltpu
 from jax.sharding import PartitionSpec as P
 
 LX = 4
@@ -47,7 +50,7 @@
     )
 
 
-def shards(fine_source, projectors, stencil_links, quark_mass):
+def shards_general(fine_source, projectors, stencil_links, quark_mass):
     comp_count = stencil_links.shape[2]
     null_count = comp_count // 2
     site_count = stencil_links.shape[1]
@@ -164,6 +167,380 @@
     )
 
 
+MESH = pl.DeviceIdType.MESH
+
+
+def flipped(number, mask, bits):
+    total = 0
+    for bit in range(bits):
+        size = 1 << bit
+        total = total + (((number // size) % 2 + (mask // size) % 2) % 2) * size
+    return total
+
+
+def widened(plane):
+    half = plane.shape[0] // 2
+    real, imag = plane[:half], plane[half:]
+    return jnp.concatenate(
+        [jnp.concatenate([real, imag], axis=1), jnp.concatenate([-imag, real], axis=1)], axis=0
+    )
+
+
+def solve_kernel(
+    count, sites, comps,
+    mass_ref, weights_ref, fine_hbm, links_hbm,
+    sol_ref, res_ref,
+    fine_ref, links_ref, near_ref, zlinks_ref, tlinks_ref, mask_ref,
+    weights_in, part_keep, part_out, part_in, sum_out, source_ref,
+    wide_ref, round_ref, halo_ref, acc_ref, basis_q, basis_p, stat_out, stat_in,
+    local_sem, wsend, wrecv, psend, precv, ssend, srecv, hsend, hrecv, gsend, grecv,
+):
+    me = lax.axis_index("ta")
+    bits = count.bit_length() - 1
+    core = me % 2
+    chip = me // 2
+    partner = chip * 2 + 1 - core
+    chips = count // 2
+    null = comps // 2
+    rows = fine_ref.shape[1]
+    rhs = fine_ref.shape[2]
+
+    fine_copy = pltpu.make_async_copy(fine_hbm, fine_ref, local_sem.at[0])
+    fine_copy.start()
+    links_copy = pltpu.make_async_copy(links_hbm, links_ref, local_sem.at[1])
+    links_copy.start()
+
+    barrier = pltpu.get_barrier_semaphore()
+
+    def greet(step, carry):
+        pl.semaphore_signal(
+            barrier, inc=1, device_id={"ta": flipped(me, step, bits)}, device_id_type=MESH
+        )
+        return carry
+
+    lax.fori_loop(1, count, greet, 0)
+    pl.semaphore_wait(barrier, count - 1)
+
+    def weights_copy(slot, other, origin):
+        return pltpu.make_async_remote_copy(
+            src_ref=weights_ref.at[slot], dst_ref=weights_in.at[origin],
+            send_sem=wsend.at[slot], recv_sem=wrecv.at[origin],
+            device_id={"ta": other}, device_id_type=MESH,
+        )
+
+    def send_weights(step, carry):
+        other = flipped(me, count - 1 - step, bits)
+        weights_copy(other, other, me).start()
+        return carry
+
+    lax.fori_loop(0, count - 1, send_weights, 0)
+
+    rows_at = lax.broadcasted_iota(jnp.int32, (rows, rhs), 0)
+    mask_ref[...] = (1 - (rows_at // null) % 2).astype(jnp.float32).astype(jnp.bfloat16)
+    links_copy.wait()
+    for site in range(sites):
+        near_ref[site] = links_ref[site, :, : 10 * comps]
+        zlinks_ref[site] = links_ref[site, :, 10 * comps : 14 * comps]
+        tlinks_ref[site] = links_ref[site, :, 14 * comps : 18 * comps]
+    fine_copy.wait()
+
+    def restricted(plane, weights):
+        fine = fine_ref[plane]
+        first = fine * mask_ref[...]
+        second = fine - first
+
+        def turned(value):
+            view = value.reshape(rows // (2 * comps), 2, comps, rhs)
+            return jnp.stack([view[:, 1], -view[:, 0]], axis=1).reshape(rows, rhs)
+
+        right = jnp.concatenate([first, second, turned(first), turned(second)], axis=1)
+        half = rows // 2
+        upper = jnp.dot(weights, right[:half], preferred_element_type=jnp.float32)
+        lower = jnp.dot(weights, right[half:], preferred_element_type=jnp.float32)
+        total = upper[:null] + lower[null:]
+        return jnp.concatenate([total[:, k * rhs : (k + 1) * rhs] for k in range(4)], axis=0)
+
+    def part_copy(slot):
+        return pltpu.make_async_remote_copy(
+            src_ref=part_out.at[slot], dst_ref=part_in.at[slot],
+            send_sem=psend.at[slot], recv_sem=precv.at[slot],
+            device_id={"ta": partner}, device_id_type=MESH,
+        )
+
+    def source_copy(slot, origin):
+        return pltpu.make_async_remote_copy(
+            src_ref=sum_out.at[slot], dst_ref=source_ref.at[origin],
+            send_sem=ssend.at[slot], recv_sem=srecv.at[origin],
+            device_id={"ta": flipped(chip, slot, bits - 1) * 2 + core}, device_id_type=MESH,
+        )
+
+    def pair(step):
+        other = flipped(chip, step, bits - 1)
+        away = other * 2 + 1 - core
+        weights_copy(me, partner, away).wait_recv()
+        part_out[step] = restricted(away, weights_in[away])
+        part_copy(step).start()
+        kept = other * 2 + core
+        weights_copy(me, partner, kept).wait_recv()
+        part_keep[step] = restricted(kept, weights_in[kept])
+
+    def finish(step):
+        part_copy(step).wait_recv()
+        sum_out[step] = part_keep[step] + part_in[step]
+        source_copy(step, chip).start()
+
+    weights_copy(me, partner, partner).wait_recv()
+    part_out[0] = restricted(partner, weights_in[partner])
+    part_copy(0).start()
+    part_keep[0] = restricted(me, weights_ref[me])
+    pair(1)
+    part_copy(0).wait_recv()
+    source_ref[chip] = part_keep[0] + part_in[0]
+
+    def pair_step(step, carry):
+        pair(step)
+        finish(step - 1)
+        return carry
+
+    lax.fori_loop(2, chips, pair_step, 0)
+    finish(chips - 1)
+
+    def source_wait(step, carry):
+        source_copy(step, flipped(chip, step, bits - 1)).wait_recv()
+        return carry
+
+    lax.fori_loop(1, chips, source_wait, 0)
+
+    mass = mass_ref[0]
+    base = (me // LZ) * LZ
+    z_at = me % LZ
+    above = base + (z_at + 1) % LZ
+    below = base + (z_at + LZ - 1) % LZ
+    other_time = (me + LZ) % count
+    targets = (other_time, above, below)
+    lines = sites // LX
+
+    def place(site, dx, dy):
+        return ((site // LX + dy) % lines) * LX + (site % LX + dx) % LX
+
+    def halo_copy(iteration, which):
+        return pltpu.make_async_remote_copy(
+            src_ref=round_ref.at[iteration], dst_ref=halo_ref.at[iteration, which],
+            send_sem=hsend.at[iteration, which], recv_sem=hrecv.at[iteration, which],
+            device_id={"ta": targets[which]}, device_id_type=MESH,
+        )
+
+    def stat_copy(iteration, other, origin):
+        return pltpu.make_async_remote_copy(
+            src_ref=stat_out.at[iteration], dst_ref=stat_in.at[iteration, origin],
+            send_sem=gsend.at[iteration, other], recv_sem=grecv.at[iteration, origin],
+            device_id={"ta": other}, device_id_type=MESH,
+        )
+
+    def times(factor, value):
+        real, imag = value[:comps], value[comps:]
+        return jnp.concatenate(
+            [factor[0] * real - factor[1] * imag, factor[0] * imag + factor[1] * real], axis=0
+        )
+
+    factors, alphas, epsilons, overlap = [], [], [], None
+    backs = []
+    for it in range(ITERS):
+        old = source_ref if it == 0 else res_ref
+        for site in range(sites):
+            round_ref[it, site] = old[site].astype(jnp.bfloat16)
+        for which in range(3):
+            halo_copy(it, which).start()
+        for site in range(sites):
+            wide_ref[site] = widened(round_ref[it, site])
+        for site in range(sites):
+            steps = ((0, 0), (1, 0), (-1, 0), (0, 1), (0, -1))
+            right = jnp.concatenate([wide_ref[place(site, dx, dy)] for dx, dy in steps], axis=0)
+            acc_ref[site] = jnp.dot(near_ref[site], right, preferred_element_type=jnp.float32)
+        halo_copy(it, 2).wait_recv()
+        halo_copy(it, 1).wait_recv()
+        for site in range(sites):
+            right = jnp.concatenate(
+                [widened(halo_ref[it, 2, site]), widened(halo_ref[it, 1, site])], axis=0
+            )
+            acc_ref[site] += jnp.dot(zlinks_ref[site], right, preferred_element_type=jnp.float32)
+        halo_copy(it, 0).wait_recv()
+        sums = [0.0] * (3 + 2 * it)
+        for site in range(sites):
+            wide = widened(halo_ref[it, 0, site])
+            right = jnp.concatenate([wide, wide], axis=0)
+            product = acc_ref[site] + jnp.dot(
+                tlinks_ref[site], right, preferred_element_type=jnp.float32
+            )
+            rounded = mass * round_ref[it, site].astype(jnp.float32)
+            q_re = product[:, :rhs] + rounded[:comps]
+            q_im = product[:, rhs:] + rounded[comps:]
+            acc_ref[site] = jnp.concatenate([q_re, q_im], axis=1)
+            r_re, r_im = old[site, :comps], old[site, comps:]
+            sums[0] += q_re * q_re + q_im * q_im
+            sums[1] += q_re * r_re + q_im * r_im
+            sums[2] += q_re * r_im - q_im * r_re
+            for j in range(it):
+                b_re, b_im = basis_q[j, site, :comps], basis_q[j, site, comps:]
+                sums[3 + 2 * j] += b_re * q_re + b_im * q_im
+                sums[4 + 2 * j] += b_re * q_im - b_im * q_re
+        lines_of = [jnp.sum(value, axis=0, keepdims=True) for value in sums]
+        lines_of += [jnp.zeros((8 - len(lines_of), rhs), jnp.float32)]
+        stats = jnp.concatenate(lines_of, axis=0)
+        stat_out[it] = stats
+
+        def send_stats(step, carry, it=it):
+            other = flipped(me, count - 1 - step, bits)
+            stat_copy(it, other, me).start()
+            return carry
+
+        lax.fori_loop(0, count - 1, send_stats, 0)
+        stat_in[it, me] = stats
+
+        def wait_stats(step, carry, it=it):
+            other = flipped(me, step, bits)
+            stat_copy(it, other, other).wait_recv()
+            return carry
+
+        lax.fori_loop(1, count, wait_stats, 0)
+        total = jnp.sum(stat_in[it], axis=0)
+        squared, cross_re, cross_im = total[0:1], total[1:2], total[2:3]
+        coefs = [(total[3 + 2 * j : 4 + 2 * j], total[4 + 2 * j : 5 + 2 * j]) for j in range(it)]
+        for j, (c_re, c_im) in enumerate(coefs):
+            squared = squared - (c_re * c_re + c_im * c_im) * (1.0 + epsilons[j])
+            cross_re = cross_re - (c_re * backs[j][0] + c_im * backs[j][1])
+            cross_im = cross_im - (c_re * backs[j][1] - c_im * backs[j][0])
+        if it == 2:
+            (a_re, a_im), (b_re, b_im) = coefs
+            pair_re, pair_im = a_re * b_re + a_im * b_im, a_re * b_im - a_im * b_re
+            squared = squared + 2.0 * (pair_re * overlap[0] - pair_im * overlap[1])
+        factor = 1.0 / jnp.sqrt(squared + 1e-06)
+        alpha = (cross_re * factor, cross_im * factor)
+        epsilon = 1e-06 * factor * factor
+        if it == 1:
+            overlap = (coefs[0][0] * epsilons[0] * factor, coefs[0][1] * epsilons[0] * factor)
+            backs[0] = (
+                backs[0][0] - (alpha[0] * overlap[0] - alpha[1] * overlap[1]),
+                backs[0][1] - (alpha[0] * overlap[1] + alpha[1] * overlap[0]),
+            )
+        backs.append((alpha[0] * epsilon, alpha[1] * epsilon))
+        epsilons.append(epsilon)
+        for site in range(sites):
+            residual = old[site]
+            q = acc_ref[site]
+            q = jnp.concatenate([q[:, :rhs], q[:, rhs:]], axis=0)
+            p = residual
+            for j in range(it):
+                q = q - times(coefs[j], basis_q[j, site])
+                p = p - times(coefs[j], basis_p[j, site])
+            q = q * factor
+            p = p * factor
+            if it < ITERS - 1:
+                basis_q[it, site] = q
+                basis_p[it, site] = p
+            step = times(alpha, p)
+            sol_ref[site] = step if it == 0 else sol_ref[site] + step
+            res_ref[site] = residual - times(alpha, q)
+
+    def drain(step, carry):
+        other = flipped(me, step, bits)
+        weights_copy(other, other, me).wait_send()
+        for it in range(ITERS):
+            stat_copy(it, other, me).wait_send()
+        return carry
+
+    lax.fori_loop(1, count, drain, 0)
+    part_copy(0).wait_send()
+
+    def drain_parts(step, carry):
+        part_copy(step).wait_send()
+        source_copy(step, chip).wait_send()
+        return carry
+
+    lax.fori_loop(1, chips, drain_parts, 0)
+    for it in range(ITERS):
+        for which in range(3):
+            halo_copy(it, which).wait_send()
+
+
+def shards_kernel(fine_source, projectors, stencil_links, quark_mass):
+    count = lax.axis_size("ta")
+    planes, local_columns, _, _, null, rhs = fine_source.shape
+    sites, comps = stencil_links.shape[1], stencil_links.shape[2]
+    rows = local_columns * 4 * null
+    fine = fine_source.reshape(planes, rows, rhs)
+    weights = projectors.reshape(count, 2, local_columns // 2, 2, null, 2, null)
+    weights = weights.transpose(0, 1, 4, 2, 5, 3, 6).reshape(count, 2 * null, rows // 2)
+    links = stencil_links.reshape(sites, comps, 18 * comps)
+    chips = count // 2
+    vector = (sites, 2 * comps, rhs)
+    f32, bf16 = jnp.float32, jnp.bfloat16
+    dma = pltpu.SemaphoreType.DMA
+    vmem = pl.BlockSpec(memory_space=pltpu.VMEM)
+    hbm = pl.BlockSpec(memory_space=pl.ANY)
+    parts = (chips, 2 * comps, rhs)
+    sol, res = pl.pallas_call(
+        functools.partial(solve_kernel, count, sites, comps),
+        out_shape=[jax.ShapeDtypeStruct(vector, f32)] * 2,
+        in_specs=[pl.BlockSpec(memory_space=pltpu.SMEM), vmem, hbm, hbm],
+        out_specs=[vmem, vmem],
+        scratch_shapes=[
+            pltpu.VMEM(fine.shape, bf16),
+            pltpu.VMEM(links.shape, bf16),
+            pltpu.VMEM((sites, comps, 10 * comps), bf16),
+            pltpu.VMEM((sites, comps, 4 * comps), bf16),
+            pltpu.VMEM((sites, comps, 4 * comps), bf16),
+            pltpu.VMEM((rows, rhs), bf16),
+            pltpu.VMEM(weights.shape, bf16),
+            pltpu.VMEM(parts, f32),
+            pltpu.VMEM(parts, f32),
+            pltpu.VMEM(parts, f32),
+            pltpu.VMEM(parts, f32),
+            pltpu.VMEM(vector, f32),
+            pltpu.VMEM((sites, 2 * comps, 2 * rhs), bf16),
+            pltpu.VMEM((ITERS, *vector), bf16),
+            pltpu.VMEM((ITERS, 3, *vector), bf16),
+            pltpu.VMEM((sites, comps, 2 * rhs), f32),
+            pltpu.VMEM((ITERS - 1, *vector), f32),
+            pltpu.VMEM((ITERS - 1, *vector), f32),
+            pltpu.VMEM((ITERS, 8, rhs), f32),
+            pltpu.VMEM((ITERS, count, 8, rhs), f32),
+            dma((2,)),
+            dma((count,)),
+            dma((count,)),
+            dma((chips,)),
+            dma((chips,)),
+            dma((chips,)),
+            dma((chips,)),
+            dma((ITERS, 3)),
+            dma((ITERS, 3)),
+            dma((ITERS, count)),
+            dma((ITERS, count)),
+        ],
+        compiler_params=pltpu.CompilerParams(
+            collective_id=0, has_side_effects=True, vmem_limit_bytes=60 * 1024 * 1024
+        ),
+    )(quark_mass, weights, fine, links)
+    return sol.reshape(1, *vector), res.reshape(1, *vector)
+
+
+def shards(fine_source, projectors, stencil_links, quark_mass):
+    count = lax.axis_size("ta")
+    sites = stencil_links.shape[1]
+    local_columns = fine_source.shape[1]
+    block = projectors.shape[1] // sites
+    fits = (
+        count == 2 * LZ
+        and count == 2 * sites
+        and count & (count - 1) == 0
+        and block == 2 * local_columns
+        and fine_source.shape[0] == count
+        and ITERS == 3
+    )
+    chosen = shards_kernel if fits else shards_general
+    return chosen(fine_source, projectors, stencil_links, quark_mass)
+
+
 def solution(mesh):
     return jax.shard_map(
         shards,

time: 335 us -> 106 us (0.32); the launches traced: 329 us -> 106 us
  waiting for transfers between devices: 106 us -> 0 us
  blocking collectives: 94.8 us -> 0 us
  Pallas kernels: 0 us -> 80.3 us
  other arithmetic: 42.2 us -> 0 us
  starting transfers between devices: 27 us -> 0 us
  local copies, waits for them, and re-layouts: 51 us -> 24.3 us
  matrix products: 5.66 us -> 0 us
    ppermute x12 -> x0, waiting for transfers between devices: 103 us -> none  [from_behind(): return lax.ppermute(value, axis, pairs)]
    psum x3 -> x0, blocking collectives: 94.8 us -> none  [shards(): lax.psum((square_loc, cross_re, cross_im, coef_re, coef_im, back_re, back...]
    pallas_call x0 -> x1, Pallas kernels: none -> 80.3 us  [shards_kernel(): pl.pallas_call(functools.partial(solve_kernel, count, sites, comps), out_...]
    another operation x10 -> x0, other arithmetic: 19.8 us -> none  [the longest x2 18.6 us: shards(): jnp.stack([upper_rows, lower_rows], axis=1)]
    ppermute x12 -> x0, starting transfers between devices: 14.8 us -> none  [from_behind(): return lax.ppermute(value, axis, pairs)]
    all_to_all x2 -> x0, starting transfers between devices: 12.2 us -> none  [the longest x1 7.64 us: shards(): lax.all_to_all(projectors, 'ta', split_axis=1, concat_axis=0, tiled=True)]
    unnamed x68 -> x2, local copies, waits for them, and re-layouts: 13.5 us -> 3.54 us
    slice x10 -> x0, local copies, waits for them, and re-layouts: 8.52 us -> none  [the longest x1 8.34 us: real_weights(): proj_im = proj_view[..., 1, :]]
  transfers between devices with their start and end apart: 14 -> 0, of which waited for: 13 -> 0; matrix products, arithmetic and copies ran while one was open for 12% -> 0% of each run, Pallas kernels for 0% -> 0%
where the time goes in v1:
time: 106 us
  Pallas kernels  80.3 us (76%)
  local copies, waits for them, and re-layouts  24.3 us (23%)
  between operations  1.3 us (1%)
    pallas_call x1, Pallas kernels, shards_kernel(): pl.pallas_call(functools.partial(solve_kernel, count, sites, comps), out_...  80.3 us
    reshape x2, local copies, waits for them, and re-layouts, shards_kernel(): weights = projectors.reshape(count, 2, local_columns // 2, 2, null, 2, null)  16.6 us
    reshape x1, local copies, waits for them, and re-layouts, shards_kernel(): weights.transpose(0, 1, 4, 2, 5, 3, 6).reshape(count, 2 * null, rows // 2)  4.15 us
    unnamed x2, local copies, waits for them, and re-layouts  3.54 us

profile of v1, /device:TPU:0, one launch (start us, length us, event | category | flops | bytes accessed | tf_op | source)
XLA Modules:
  0.0 105.9 jit_solution(299960671615627037)
XLA Ops:
  0.6 11.4 %reshape.22 = bf16[16,2,4,2,24,2,24]{6,5,4,3,2,1,0:T(2,128)(2,1)} reshape(bf16[1,128,2304]{2,1,0:T(8,128)(2,1)} %param.5) | data formatting | bytes 1179648 | tf_op jit(solution)/shard_map/reshape | solution.py:472
  12.1 5.2 %copy.8 = bf16[16,2,4,2,24,2,24]{6,3,5,2,4,1,0:T(2,128)(2,1)S(1)} copy(bf16[16,2,4,2,24,2,24]{6,5,4,3,2,1,0:T(2,128)(2,1)} %reshape.22) | data formatting | bytes 1179648 | tf_op jit(solution)/shard_map/reshape | solution.py:472
  17.3 4.2 %reshape.23.weights_ref = bf16[16,48,384]{2,1,0:T(8,128)(2,1)} reshape(bf16[16,2,24,4,2,2,24]{6,5,4,3,2,1,0:T(2,128)(2,1)S(1)} %bitcast.7) | data formatting | bytes 1179648 | tf_op jit(solution)/shard_map/reshape | solution.py:473
  22.1 80.3 %shard_map.59 = (f32[8,96,128]{2,1,0:T(8,128)}, f32[8,96,128]{2,1,0:T(8,128)}) custom-call(f32[1]{0:T(128)S(6)} %copy.11.mass_ref, bf16[16,48,384]{2,1,0:T(8,128)(2,1)} %reshape.23.weights_ref, bf16[16,768,128]{2,1,0:T(8,128)(2,1)} %bitcast.8, bf16[8,48,864]{2,1,0:T(8,128)(2,1)} %bitcast.9), custom_call_target="tpu_custom_call" | custom-call | tf_op jit(solution)/shard_map/pallas_call | solution.py:482
  102.4 1.8 %copy.12 = f32[1,8,96,128]{3,2,1,0:T(8,128)} copy(f32[1,8,96,128]{3,2,1,0:T(8,128)} %bitcast.11) | data formatting | bytes 786432
  104.2 1.8 %copy.13 = f32[1,8,96,128]{3,2,1,0:T(8,128)} copy(f32[1,8,96,128]{3,2,1,0:T(8,128)} %bitcast.10) | data formatting | bytes 786432

commit v2 on v1

--- a/solution.py
+++ b/solution.py
@@ -188,10 +188,10 @@
 
 def solve_kernel(
     count, sites, comps,
-    mass_ref, weights_ref, fine_hbm, links_hbm,
+    mass_ref, proj_ref, fine_hbm, links_hbm,
     sol_ref, res_ref,
-    fine_ref, links_ref, near_ref, zlinks_ref, tlinks_ref, mask_ref,
-    weights_in, part_keep, part_out, part_in, sum_out, source_ref,
+    fine_ref, links_ref, near_ref, zlinks_ref, tlinks_ref, fold_ref,
+    weights_ref, weights_in, part_keep, part_out, part_in, sum_out, source_ref,
     wide_ref, round_ref, halo_ref, acc_ref, basis_q, basis_p, stat_out, stat_in,
     local_sem, wsend, wrecv, psend, precv, ssend, srecv, hsend, hrecv, gsend, grecv,
 ):
@@ -228,15 +228,40 @@
             device_id={"ta": other}, device_id_type=MESH,
         )
 
+    columns = proj_ref.shape[1]
+    width = columns * comps
+    groups = comps // columns
+    lane_at = lax.broadcasted_iota(jnp.int32, (columns, width), 1) // comps
+    row_at = lax.broadcasted_iota(jnp.int32, (columns, width), 0)
+    picks = (lane_at == row_at).astype(jnp.float32)
+    fold_row = lax.broadcasted_iota(jnp.int32, (width, width), 0) % comps
+    fold_lane = lax.broadcasted_iota(jnp.int32, (width, width), 1) % comps
+    fold_ref[...] = (fold_row == fold_lane).astype(jnp.float32).astype(jnp.bfloat16)
+
+    def arrange(slot):
+        raw = proj_ref[slot].astype(jnp.float32)
+        pieces = []
+        for column in range(columns):
+            for group in range(groups):
+                row = raw[column : column + 1, group * width : (group + 1) * width]
+                pieces.append(row * picks)
+        left = jnp.concatenate(pieces, axis=0).astype(jnp.bfloat16)
+        spread = jnp.dot(left, fold_ref[...], preferred_element_type=jnp.float32)
+        total = spread[:comps] * picks[0:1]
+        for column in range(1, columns):
+            block = spread[column * comps : (column + 1) * comps]
+            total = total + block * picks[column : column + 1]
+        weights_ref[slot] = total.astype(jnp.bfloat16)
+
     def send_weights(step, carry):
         other = flipped(me, count - 1 - step, bits)
+        arrange(other)
         weights_copy(other, other, me).start()
         return carry
 
     lax.fori_loop(0, count - 1, send_weights, 0)
-
-    rows_at = lax.broadcasted_iota(jnp.int32, (rows, rhs), 0)
-    mask_ref[...] = (1 - (rows_at // null) % 2).astype(jnp.float32).astype(jnp.bfloat16)
+    arrange(me)
+
     links_copy.wait()
     for site in range(sites):
         near_ref[site] = links_ref[site, :, : 10 * comps]
@@ -245,20 +270,25 @@
     fine_copy.wait()
 
     def restricted(plane, weights):
-        fine = fine_ref[plane]
-        first = fine * mask_ref[...]
-        second = fine - first
-
-        def turned(value):
-            view = value.reshape(rows // (2 * comps), 2, comps, rhs)
-            return jnp.stack([view[:, 1], -view[:, 0]], axis=1).reshape(rows, rhs)
-
-        right = jnp.concatenate([first, second, turned(first), turned(second)], axis=1)
-        half = rows // 2
-        upper = jnp.dot(weights, right[:half], preferred_element_type=jnp.float32)
-        lower = jnp.dot(weights, right[half:], preferred_element_type=jnp.float32)
-        total = upper[:null] + lower[null:]
-        return jnp.concatenate([total[:, k * rhs : (k + 1) * rhs] for k in range(4)], axis=0)
+        fine = fine_ref[plane].astype(jnp.float32).reshape(columns, 2, 2, null, rhs)
+
+        def ordered(real, imag, half):
+            view = jnp.stack([real[:, half], imag[:, half]], axis=1)
+            return view.reshape(width, rhs).astype(jnp.bfloat16)
+
+        real, imag = fine[:, 0], fine[:, 1]
+        right = jnp.concatenate(
+            [ordered(real, imag, 0), ordered(real, imag, 1),
+             ordered(imag, -real, 0), ordered(imag, -real, 1)], axis=1
+        )
+        total = jnp.dot(weights, right, preferred_element_type=jnp.float32)
+        return jnp.concatenate(
+            [
+                total[:null, :rhs], total[null:, rhs : 2 * rhs],
+                total[:null, 2 * rhs : 3 * rhs], total[null:, 3 * rhs :],
+            ],
+            axis=0,
+        )
 
     def part_copy(slot):
         return pltpu.make_async_remote_copy(
@@ -469,8 +499,8 @@
     sites, comps = stencil_links.shape[1], stencil_links.shape[2]
     rows = local_columns * 4 * null
     fine = fine_source.reshape(planes, rows, rhs)
-    weights = projectors.reshape(count, 2, local_columns // 2, 2, null, 2, null)
-    weights = weights.transpose(0, 1, 4, 2, 5, 3, 6).reshape(count, 2 * null, rows // 2)
+    proj = projectors.reshape(count, local_columns, 4 * null * null)
+    width = local_columns * comps
     links = stencil_links.reshape(sites, comps, 18 * comps)
     chips = count // 2
     vector = (sites, 2 * comps, rhs)
@@ -490,8 +520,9 @@
             pltpu.VMEM((sites, comps, 10 * comps), bf16),
             pltpu.VMEM((sites, comps, 4 * comps), bf16),
             pltpu.VMEM((sites, comps, 4 * comps), bf16),
-            pltpu.VMEM((rows, rhs), bf16),
-            pltpu.VMEM(weights.shape, bf16),
+            pltpu.VMEM((width, width), bf16),
+            pltpu.VMEM((count, comps, width), bf16),
+            pltpu.VMEM((count, comps, width), bf16),
             pltpu.VMEM(parts, f32),
             pltpu.VMEM(parts, f32),
             pltpu.VMEM(parts, f32),
@@ -520,7 +551,7 @@
         compiler_params=pltpu.CompilerParams(
             collective_id=0, has_side_effects=True, vmem_limit_bytes=60 * 1024 * 1024
         ),
-    )(quark_mass, weights, fine, links)
+    )(quark_mass, proj, fine, links)
     return sol.reshape(1, *vector), res.reshape(1, *vector)
 
 
@@ -534,6 +565,7 @@
         and count == 2 * sites
         and count & (count - 1) == 0
         and block == 2 * local_columns
+        and stencil_links.shape[2] % local_columns == 0
         and fine_source.shape[0] == count
         and ITERS == 3
     )

time: 106 us -> 84.3 us (0.80)
  local copies, waits for them, and re-layouts: 24.3 us -> 3.54 us
  Pallas kernels: 80.3 us -> 79.2 us
    reshape x3 -> x0, local copies, waits for them, and re-layouts: 20.8 us -> none  [the longest x2 16.6 us: shards_kernel(): weights = projectors.reshape(count, 2, local_columns // 2, 2, null, 2, null)]
where the time goes in v2:
time: 84.3 us; the launch traced here: 84.1 us
  Pallas kernels  79.2 us (94%)
  local copies, waits for them, and re-layouts  3.54 us (4%)
  between operations  1.29 us (2%)
    pallas_call x1, Pallas kernels, shards_kernel(): pl.pallas_call(functools.partial(solve_kernel, count, sites, comps), out_...  79.2 us
    unnamed x2, local copies, waits for them, and re-layouts  3.54 us

profile of v2, /device:TPU:0, one launch (start us, length us, event | category | flops | bytes accessed | tf_op | source)
XLA Modules:
  0.0 84.1 jit_solution(479381696708980266)
XLA Ops:
  1.3 79.2 %shard_map.59 = (f32[8,96,128]{2,1,0:T(8,128)}, f32[8,96,128]{2,1,0:T(8,128)}) custom-call(f32[1]{0:T(128)S(6)} %copy.8.mass_ref, bf16[16,8,2304]{2,1,0:T(8,128)(2,1)} %bitcast.7, bf16[16,768,128]{2,1,0:T(8,128)(2,1)} %bitcast.5, bf16[8,48,864]{2,1,0:T(8,128)(2,1)} %bitcast.6), custom_call_target="tpu_custom_call" | custom-call | tf_op jit(solution)/shard_map/pallas_call | solution.py:512
  80.5 1.8 %copy.9 = f32[1,8,96,128]{3,2,1,0:T(8,128)} copy(f32[1,8,96,128]{3,2,1,0:T(8,128)} %bitcast.9) | data formatting | bytes 786432
  82.3 1.8 %copy.10 = f32[1,8,96,128]{3,2,1,0:T(8,128)} copy(f32[1,8,96,128]{3,2,1,0:T(8,128)} %bitcast.8) | data formatting | bytes 786432

commit v3 on v2

--- a/solution.py
+++ b/solution.py
@@ -178,12 +178,27 @@
     return total
 
 
-def widened(plane):
-    half = plane.shape[0] // 2
-    real, imag = plane[:half], plane[half:]
+def swapped(value):
+    return pltpu.roll(value, value.shape[-1] // 2, value.ndim - 1)
+
+
+def lower_lanes(shape):
+    return lax.broadcasted_iota(jnp.int32, shape, len(shape) - 1) < shape[-1] // 2
+
+
+def turned(value):
+    other = swapped(value)
+    return jnp.where(lower_lanes(value.shape), -other, other)
+
+
+def widened(rounded):
     return jnp.concatenate(
-        [jnp.concatenate([real, imag], axis=1), jnp.concatenate([-imag, real], axis=1)], axis=0
-    )
+        [rounded, turned(rounded.astype(jnp.float32)).astype(jnp.bfloat16)], axis=0
+    )
+
+
+def times(factor, value):
+    return factor[0] * value + factor[1] * turned(value)
 
 
 def solve_kernel(
@@ -192,7 +207,7 @@
     sol_ref, res_ref,
     fine_ref, links_ref, near_ref, zlinks_ref, tlinks_ref, fold_ref,
     weights_ref, weights_in, part_keep, part_out, part_in, sum_out, source_ref,
-    wide_ref, round_ref, halo_ref, acc_ref, basis_q, basis_p, stat_out, stat_in,
+    wide_ref, round_ref, halo_ref, acc_ref, sol_half, res_half, basis_q, basis_p, stat_out, stat_in,
     local_sem, wsend, wrecv, psend, precv, ssend, srecv, hsend, hrecv, gsend, grecv,
 ):
     me = lax.axis_index("ta")
@@ -201,6 +216,11 @@
     chip = me // 2
     partner = chip * 2 + 1 - core
     chips = count // 2
+    turns = [(1 - 2 * ((me // (1 << bit)) % 2)) * (1 << bit) for bit in range(bits)]
+    others = [me]
+    for step in range(1, count):
+        top = step.bit_length() - 1
+        others.append(others[step - (1 << top)] + turns[top])
     null = comps // 2
     rows = fine_ref.shape[1]
     rhs = fine_ref.shape[2]
@@ -212,13 +232,8 @@
 
     barrier = pltpu.get_barrier_semaphore()
 
-    def greet(step, carry):
-        pl.semaphore_signal(
-            barrier, inc=1, device_id={"ta": flipped(me, step, bits)}, device_id_type=MESH
-        )
-        return carry
-
-    lax.fori_loop(1, count, greet, 0)
+    for other in others[1:]:
+        pl.semaphore_signal(barrier, inc=1, device_id={"ta": other}, device_id_type=MESH)
     pl.semaphore_wait(barrier, count - 1)
 
     def weights_copy(slot, other, origin):
@@ -282,12 +297,13 @@
              ordered(imag, -real, 0), ordered(imag, -real, 1)], axis=1
         )
         total = jnp.dot(weights, right, preferred_element_type=jnp.float32)
-        return jnp.concatenate(
-            [
-                total[:null, :rhs], total[null:, rhs : 2 * rhs],
-                total[:null, 2 * rhs : 3 * rhs], total[null:, 3 * rhs :],
-            ],
-            axis=0,
+        real = jnp.concatenate([total[:null, :rhs], total[null:, rhs : 2 * rhs]], axis=0)
+        imag = jnp.concatenate(
+            [total[:null, 2 * rhs : 3 * rhs], total[null:, 3 * rhs :]], axis=0
+        )
+        low = lower_lanes(real.shape)
+        return jnp.stack(
+            [jnp.where(low, real, swapped(imag)), jnp.where(low, swapped(real), imag)], axis=0
         )
 
     def part_copy(slot):
@@ -335,11 +351,8 @@
     lax.fori_loop(2, chips, pair_step, 0)
     finish(chips - 1)
 
-    def source_wait(step, carry):
-        source_copy(step, flipped(chip, step, bits - 1)).wait_recv()
-        return carry
-
-    lax.fori_loop(1, chips, source_wait, 0)
+    for step in range(1, chips):
+        source_copy(step, others[2 * step] // 2).wait_recv()
 
     mass = mass_ref[0]
     base = (me // LZ) * LZ
@@ -353,89 +366,94 @@
     def place(site, dx, dy):
         return ((site // LX + dy) % lines) * LX + (site % LX + dx) % LX
 
-    def halo_copy(iteration, which):
+    def halo_copy(it, half, which):
         return pltpu.make_async_remote_copy(
-            src_ref=round_ref.at[iteration], dst_ref=halo_ref.at[iteration, which],
-            send_sem=hsend.at[iteration, which], recv_sem=hrecv.at[iteration, which],
+            src_ref=round_ref.at[it, half], dst_ref=halo_ref.at[it, half, which],
+            send_sem=hsend.at[it, half, which], recv_sem=hrecv.at[it, half, which],
             device_id={"ta": targets[which]}, device_id_type=MESH,
         )
 
-    def stat_copy(iteration, other, origin):
+    def stat_copy(it, half, other, origin):
         return pltpu.make_async_remote_copy(
-            src_ref=stat_out.at[iteration], dst_ref=stat_in.at[iteration, origin],
-            send_sem=gsend.at[iteration, other], recv_sem=grecv.at[iteration, origin],
+            src_ref=stat_out.at[it, half], dst_ref=stat_in.at[it, half, origin],
+            send_sem=gsend.at[it, half, other], recv_sem=grecv.at[it, half, origin],
             device_id={"ta": other}, device_id_type=MESH,
         )
 
-    def times(factor, value):
-        real, imag = value[:comps], value[comps:]
-        return jnp.concatenate(
-            [factor[0] * real - factor[1] * imag, factor[0] * imag + factor[1] * real], axis=0
-        )
-
-    factors, alphas, epsilons, overlap = [], [], [], None
-    backs = []
-    for it in range(ITERS):
-        old = source_ref if it == 0 else res_ref
+    def residual_at(it, half, site):
+        return source_ref[site, half] if it == 0 else res_half[half, site]
+
+    def send_halo(it, half):
         for site in range(sites):
-            round_ref[it, site] = old[site].astype(jnp.bfloat16)
+            round_ref[it, half, site] = residual_at(it, half, site).astype(jnp.bfloat16)
         for which in range(3):
-            halo_copy(it, which).start()
+            halo_copy(it, half, which).start()
+
+    def near_product(it, half):
         for site in range(sites):
-            wide_ref[site] = widened(round_ref[it, site])
-        for site in range(sites):
-            steps = ((0, 0), (1, 0), (-1, 0), (0, 1), (0, -1))
-            right = jnp.concatenate([wide_ref[place(site, dx, dy)] for dx, dy in steps], axis=0)
-            acc_ref[site] = jnp.dot(near_ref[site], right, preferred_element_type=jnp.float32)
-        halo_copy(it, 2).wait_recv()
-        halo_copy(it, 1).wait_recv()
+            wide_ref[half, site] = widened(round_ref[it, half, site])
+        steps = ((0, 0), (1, 0), (-1, 0), (0, 1), (0, -1))
         for site in range(sites):
             right = jnp.concatenate(
-                [widened(halo_ref[it, 2, site]), widened(halo_ref[it, 1, site])], axis=0
-            )
-            acc_ref[site] += jnp.dot(zlinks_ref[site], right, preferred_element_type=jnp.float32)
-        halo_copy(it, 0).wait_recv()
+                [wide_ref[half, place(site, dx, dy)] for dx, dy in steps], axis=0
+            )
+            acc_ref[half, site] = jnp.dot(
+                near_ref[site], right, preferred_element_type=jnp.float32
+            )
+
+    def far_product(it, half):
+        halo_copy(it, half, 2).wait_recv()
+        halo_copy(it, half, 1).wait_recv()
+        for site in range(sites):
+            right = jnp.concatenate(
+                [widened(halo_ref[it, half, 2, site]), widened(halo_ref[it, half, 1, site])],
+                axis=0,
+            )
+            acc_ref[half, site] += jnp.dot(
+                zlinks_ref[site], right, preferred_element_type=jnp.float32
+            )
+        halo_copy(it, half, 0).wait_recv()
         sums = [0.0] * (3 + 2 * it)
         for site in range(sites):
-            wide = widened(halo_ref[it, 0, site])
+            wide = widened(halo_ref[it, half, 0, site])
             right = jnp.concatenate([wide, wide], axis=0)
-            product = acc_ref[site] + jnp.dot(
+            product = acc_ref[half, site] + jnp.dot(
                 tlinks_ref[site], right, preferred_element_type=jnp.float32
             )
-            rounded = mass * round_ref[it, site].astype(jnp.float32)
-            q_re = product[:, :rhs] + rounded[:comps]
-            q_im = product[:, rhs:] + rounded[comps:]
-            acc_ref[site] = jnp.concatenate([q_re, q_im], axis=1)
-            r_re, r_im = old[site, :comps], old[site, comps:]
-            sums[0] += q_re * q_re + q_im * q_im
-            sums[1] += q_re * r_re + q_im * r_im
-            sums[2] += q_re * r_im - q_im * r_re
+            q = product + mass * round_ref[it, half, site].astype(jnp.float32)
+            acc_ref[half, site] = q
+            r = residual_at(it, half, site)
+            q_other = swapped(q)
+            sums[0] += q * q
+            sums[1] += q * r
+            sums[2] += q * swapped(r)
             for j in range(it):
-                b_re, b_im = basis_q[j, site, :comps], basis_q[j, site, comps:]
-                sums[3 + 2 * j] += b_re * q_re + b_im * q_im
-                sums[4 + 2 * j] += b_re * q_im - b_im * q_re
+                b = basis_q[j, half, site]
+                sums[3 + 2 * j] += b * q
+                sums[4 + 2 * j] += b * q_other
         lines_of = [jnp.sum(value, axis=0, keepdims=True) for value in sums]
         lines_of += [jnp.zeros((8 - len(lines_of), rhs), jnp.float32)]
         stats = jnp.concatenate(lines_of, axis=0)
-        stat_out[it] = stats
-
-        def send_stats(step, carry, it=it):
-            other = flipped(me, count - 1 - step, bits)
-            stat_copy(it, other, me).start()
-            return carry
-
-        lax.fori_loop(0, count - 1, send_stats, 0)
-        stat_in[it, me] = stats
-
-        def wait_stats(step, carry, it=it):
-            other = flipped(me, step, bits)
-            stat_copy(it, other, other).wait_recv()
-            return carry
-
-        lax.fori_loop(1, count, wait_stats, 0)
-        total = jnp.sum(stat_in[it], axis=0)
-        squared, cross_re, cross_im = total[0:1], total[1:2], total[2:3]
-        coefs = [(total[3 + 2 * j : 4 + 2 * j], total[4 + 2 * j : 5 + 2 * j]) for j in range(it)]
+        stat_out[it, half] = stats
+
+        for other in others[:0:-1]:
+            stat_copy(it, half, other, me).start()
+        stat_in[it, half, me] = stats
+
+    scalars = [([], [], [], []) for _ in range(2)]
+
+    def update(it, half):
+        for other in others[1:]:
+            stat_copy(it, half, other, other).wait_recv()
+        total = jnp.sum(stat_in[it, half], axis=0)
+        moved = swapped(total)
+        reals = total + moved
+        imags = jnp.where(lower_lanes(total.shape), total - moved, moved - total)
+        backs, epsilons, overlaps, _ = scalars[half]
+        squared, cross_re, cross_im = reals[0:1], reals[1:2], imags[2:3]
+        coefs = [
+            (reals[3 + 2 * j : 4 + 2 * j], imags[4 + 2 * j : 5 + 2 * j]) for j in range(it)
+        ]
         for j, (c_re, c_im) in enumerate(coefs):
             squared = squared - (c_re * c_re + c_im * c_im) * (1.0 + epsilons[j])
             cross_re = cross_re - (c_re * backs[j][0] + c_im * backs[j][1])
@@ -443,54 +461,68 @@
         if it == 2:
             (a_re, a_im), (b_re, b_im) = coefs
             pair_re, pair_im = a_re * b_re + a_im * b_im, a_re * b_im - a_im * b_re
-            squared = squared + 2.0 * (pair_re * overlap[0] - pair_im * overlap[1])
+            squared = squared + 2.0 * (pair_re * overlaps[0][0] - pair_im * overlaps[0][1])
         factor = 1.0 / jnp.sqrt(squared + 1e-06)
         alpha = (cross_re * factor, cross_im * factor)
         epsilon = 1e-06 * factor * factor
         if it == 1:
-            overlap = (coefs[0][0] * epsilons[0] * factor, coefs[0][1] * epsilons[0] * factor)
+            over = (coefs[0][0] * epsilons[0] * factor, coefs[0][1] * epsilons[0] * factor)
+            overlaps.append(over)
             backs[0] = (
-                backs[0][0] - (alpha[0] * overlap[0] - alpha[1] * overlap[1]),
-                backs[0][1] - (alpha[0] * overlap[1] + alpha[1] * overlap[0]),
+                backs[0][0] - (alpha[0] * over[0] - alpha[1] * over[1]),
+                backs[0][1] - (alpha[0] * over[1] + alpha[1] * over[0]),
             )
         backs.append((alpha[0] * epsilon, alpha[1] * epsilon))
         epsilons.append(epsilon)
         for site in range(sites):
-            residual = old[site]
-            q = acc_ref[site]
-            q = jnp.concatenate([q[:, :rhs], q[:, rhs:]], axis=0)
+            residual = residual_at(it, half, site)
+            q = acc_ref[half, site]
             p = residual
             for j in range(it):
-                q = q - times(coefs[j], basis_q[j, site])
-                p = p - times(coefs[j], basis_p[j, site])
+                q = q - times(coefs[j], basis_q[j, half, site])
+                p = p - times(coefs[j], basis_p[j, half, site])
             q = q * factor
             p = p * factor
             if it < ITERS - 1:
-                basis_q[it, site] = q
-                basis_p[it, site] = p
+                basis_q[it, half, site] = q
+                basis_p[it, half, site] = p
             step = times(alpha, p)
-            sol_ref[site] = step if it == 0 else sol_ref[site] + step
-            res_ref[site] = residual - times(alpha, q)
-
-    def drain(step, carry):
-        other = flipped(me, step, bits)
+            sol_half[half, site] = step if it == 0 else sol_half[half, site] + step
+            res_half[half, site] = residual - times(alpha, q)
+
+    for half in range(2):
+        send_halo(0, half)
+    for half in range(2):
+        near_product(0, half)
+    for it in range(ITERS):
+        for half in range(2):
+            far_product(it, half)
+        for half in range(2):
+            update(it, half)
+            if it < ITERS - 1:
+                send_halo(it + 1, half)
+                near_product(it + 1, half)
+    for from_ref, to_ref in ((sol_half, sol_ref), (res_half, res_ref)):
+        for site in range(sites):
+            first, second = from_ref[0, site], from_ref[1, site]
+            low = lower_lanes(first.shape)
+            to_ref[site, :comps] = jnp.where(low, first, swapped(second))
+            to_ref[site, comps:] = jnp.where(low, swapped(first), second)
+
+    for other in others[1:]:
         weights_copy(other, other, me).wait_send()
         for it in range(ITERS):
-            stat_copy(it, other, me).wait_send()
-        return carry
-
-    lax.fori_loop(1, count, drain, 0)
+            for half in range(2):
+                stat_copy(it, half, other, me).wait_send()
     part_copy(0).wait_send()
 
-    def drain_parts(step, carry):
+    for step in range(1, chips):
         part_copy(step).wait_send()
         source_copy(step, chip).wait_send()
-        return carry
-
-    lax.fori_loop(1, chips, drain_parts, 0)
     for it in range(ITERS):
-        for which in range(3):
-            halo_copy(it, which).wait_send()
+        for half in range(2):
+            for which in range(3):
+                halo_copy(it, half, which).wait_send()
 
 
 def shards_kernel(fine_source, projectors, stencil_links, quark_mass):
@@ -508,7 +540,8 @@
     dma = pltpu.SemaphoreType.DMA
     vmem = pl.BlockSpec(memory_space=pltpu.VMEM)
     hbm = pl.BlockSpec(memory_space=pl.ANY)
-    parts = (chips, 2 * comps, rhs)
+    parts = (chips, 2, comps, rhs)
+    half = (sites, comps, rhs)
     sol, res = pl.pallas_call(
         functools.partial(solve_kernel, count, sites, comps),
         out_shape=[jax.ShapeDtypeStruct(vector, f32)] * 2,
@@ -527,15 +560,17 @@
             pltpu.VMEM(parts, f32),
             pltpu.VMEM(parts, f32),
             pltpu.VMEM(parts, f32),
-            pltpu.VMEM(vector, f32),
-            pltpu.VMEM((sites, 2 * comps, 2 * rhs), bf16),
-            pltpu.VMEM((ITERS, *vector), bf16),
-            pltpu.VMEM((ITERS, 3, *vector), bf16),
-            pltpu.VMEM((sites, comps, 2 * rhs), f32),
-            pltpu.VMEM((ITERS - 1, *vector), f32),
-            pltpu.VMEM((ITERS - 1, *vector), f32),
-            pltpu.VMEM((ITERS, 8, rhs), f32),
-            pltpu.VMEM((ITERS, count, 8, rhs), f32),
+            pltpu.VMEM((sites, 2, comps, rhs), f32),
+            pltpu.VMEM((2, sites, 2 * comps, rhs), bf16),
+            pltpu.VMEM((ITERS, 2, *half), bf16),
+            pltpu.VMEM((ITERS, 2, 3, *half), bf16),
+            pltpu.VMEM((2, *half), f32),
+            pltpu.VMEM((2, *half), f32),
+            pltpu.VMEM((2, *half), f32),
+            pltpu.VMEM((ITERS - 1, 2, *half), f32),
+            pltpu.VMEM((ITERS - 1, 2, *half), f32),
+            pltpu.VMEM((ITERS, 2, 8, rhs), f32),
+            pltpu.VMEM((ITERS, 2, count, 8, rhs), f32),
             dma((2,)),
             dma((count,)),
             dma((count,)),
@@ -543,10 +578,10 @@
             dma((chips,)),
             dma((chips,)),
             dma((chips,)),
-            dma((ITERS, 3)),
-            dma((ITERS, 3)),
-            dma((ITERS, count)),
-            dma((ITERS, count)),
+            dma((ITERS, 2, 3)),
+            dma((ITERS, 2, 3)),
+            dma((ITERS, 2, count)),
+            dma((ITERS, 2, count)),
         ],
         compiler_params=pltpu.CompilerParams(
             collective_id=0, has_side_effects=True, vmem_limit_bytes=60 * 1024 * 1024
@@ -568,6 +603,7 @@
         and stencil_links.shape[2] % local_columns == 0
         and fine_source.shape[0] == count
         and ITERS == 3
+        and fine_source.shape[5] % 2 == 0
     )
     chosen = shards_kernel if fits else shards_general
     return chosen(fine_source, projectors, stencil_links, quark_mass)

time: 84.3 us -> 83.6 us (level)
  no operation moved by 1% of the time
where the time goes in v3:
time: 83.6 us; the launch traced here: 83.4 us
  Pallas kernels  78.6 us (94%)
  local copies, waits for them, and re-layouts  3.54 us (4%)
  between operations  1.29 us (2%)
    pallas_call x1, Pallas kernels, shards_kernel(): pl.pallas_call(functools.partial(solve_kernel, count, sites, comps), out_...  78.6 us
    unnamed x2, local copies, waits for them, and re-layouts  3.54 us

profile of v3, /device:TPU:0, one launch (start us, length us, event | category | flops | bytes accessed | tf_op | source)
XLA Modules:
  0.0 83.4 jit_solution(18098745175990517030)
XLA Ops:
  1.3 78.6 %shard_map.59 = (f32[8,96,128]{2,1,0:T(8,128)}, f32[8,96,128]{2,1,0:T(8,128)}) custom-call(f32[1]{0:T(128)S(6)} %copy.8.mass_ref, bf16[16,8,2304]{2,1,0:T(8,128)(2,1)} %bitcast.7, bf16[16,768,128]{2,1,0:T(8,128)(2,1)} %bitcast.5, bf16[8,48,864]{2,1,0:T(8,128)(2,1)} %bitcast.6), custom_call_target="tpu_custom_call" | custom-call | tf_op jit(solution)/shard_map/pallas_call | solution.py:545
  79.8 1.8 %copy.9 = f32[1,8,96,128]{3,2,1,0:T(8,128)} copy(f32[1,8,96,128]{3,2,1,0:T(8,128)} %bitcast.9) | data formatting | bytes 786432
  81.6 1.8 %copy.10 = f32[1,8,96,128]{3,2,1,0:T(8,128)} copy(f32[1,8,96,128]{3,2,1,0:T(8,128)} %bitcast.8) | data formatting | bytes 786432
